TPU v7x, 32 devices: a whole 2x2x4 slice. The times are simulated.
32 devices in a mesh: seq: 8 (over z, x), head: 2 (over y), dp: 2 (over core).
Axes of the slice: x: 2, y: 2, z: 4, core: 2. Of those that a mesh axis runs over, the one named last changes fastest.
Arguments:
- queries: bfloat16 [8192, 4096], P(('dp', 'seq'), 'head'), parts along dimension 0, may hold values from -200 to 200
- keys: bfloat16 [8192, 1024], P(('dp', 'seq'), 'head'), parts along dimension 0, may hold values from -4 to 4
- values: bfloat16 [8192, 1024], P(('dp', 'seq'), 'head'), parts along dimension 0, may hold values from -15 to 15
- doc_ids: int32 [8192], P(('dp', 'seq')), parts along dimension 0, may hold values from 0 to 7, as said below
- block_lists: int32 [64, 16], P(('dp', 'seq')), parts along dimension 0, may hold values from 0 to 32, as said below
- w_out: bfloat16 [4096, 4096], P('head'), may hold values from -0.09375 to 0.09375
Outputs:
- mixed: bfloat16 [8192, 4096], P(('dp', 'seq'), 'head'), parts along dimension 0
There are 2 independent parts, one for each index of `dp`. A program takes and returns all parts, laid end to end along the dimension named above; an argument that names none is the same for every part. Nothing has to cross between parts.
Inputs may be any that keep to these rules, and one draw needn't show every extreme that they name: `block_lists`: row i lists the blocks that query block i reads: 16 entries, each a block of the sequence or the null value 32; the non-null entries of a row are distinct and include i. Blocks k * 4 to k * 4 + 3 lie on index k of seq; over the rows of one index of seq together, at most one distinct block of each other index of seq is named (so each index of seq sends at most one of its blocks to each other index). `doc_ids`: never falling along the sequence.
All inputs are finite; a program needn't handle non-finite values.
Results may differ from a plain program's by a relative error of at most 0.013.
Values may be sent and summed in bfloat16 or wider, within the bound.
A program may use at most 128 MiB of HBM per device.

v0:
```python
import functools
import math

import jax
import jax.numpy as jnp
from jax import lax
from jax.experimental import pallas as pl
from jax.experimental.pallas import tpu as pltpu
from jax.sharding import PartitionSpec as P

HEAD_SIZE = 128
BLOCK = 128
LANES = 128
DOCS = 8
GROUP = 4
PIECES = 2
TILE = 512
MESH = pl.DeviceIdType.MESH

far_score = float(2**20)
exp2_scale = math.log2(math.e) / math.sqrt(HEAD_SIZE)


def column_of(row):
    return jnp.broadcast_to(row, (BLOCK, LANES)).astype(jnp.float32).T


def kernel(
    seq_count,
    head_count,
    dp_count,
    lists_ref,
    docs_ref,
    q_hbm,
    k_hbm,
    v_hbm,
    w_hbm,
    out_hbm,
    q_ref,
    k_ref,
    v_ref,
    w_ref,
    note_out,
    note_in,
    stage,
    land,
    qext,
    kext,
    scores,
    probs,
    attn,
    ysend,
    yrecv,
    kept,
    done,
    load_sem,
    note_ssem,
    note_rsem,
    kv_ssem,
    kv_rsem,
    y_ssem,
    y_rsem,
    out_sem,
    turn_sem,
):
    own = lax.axis_index("seq")
    head = lax.axis_index("head")
    core = lax.axis_index("dp")
    blocks = docs_ref.shape[0]
    slots = blocks + seq_count - 1
    kv_heads = k_ref.shape[1] // HEAD_SIZE
    width = GROUP * HEAD_SIZE
    cols = kept.shape[1]
    piece = cols // PIECES
    tile = min(TILE, piece)
    others = head_count - 1

    loads = [
        pltpu.make_async_copy(src, dst, load_sem.at[n])
        for n, (src, dst) in enumerate(
            ((k_hbm, k_ref), (v_hbm, v_ref), (q_hbm, q_ref), (w_hbm, w_ref))
        )
    ]
    for load in loads:
        load.start()

    barrier = pltpu.get_barrier_semaphore()
    for d in range(1, seq_count):
        pl.semaphore_signal(
            barrier, inc=1, device_id={"seq": lax.rem(own + d, seq_count)}, device_id_type=MESH
        )
    for d in range(1, head_count):
        pl.semaphore_signal(
            barrier, inc=1, device_id={"head": lax.rem(head + d, head_count)}, device_id_type=MESH
        )
    for d in range(1, dp_count):
        pl.semaphore_signal(
            barrier, inc=1, device_id={"dp": lax.rem(core + d, dp_count)}, device_id_type=MESH
        )

    lane = lax.broadcasted_iota(jnp.int32, (1, LANES), 1)
    slot = lane - DOCS
    source = own - (slot - blocks + 1)
    source = jnp.where(source < 0, source + seq_count, source)
    is_own = (slot >= 0) & (slot < blocks)
    is_far = (slot >= blocks) & (slot < slots)
    low = jnp.where(is_own, own * blocks + slot, jnp.where(is_far, source * blocks, -1))
    high = jnp.where(is_own, low + 1, jnp.where(is_far, low + blocks, -1))
    owner_low = lane * blocks
    asked = jnp.zeros((1, LANES), jnp.int32)
    listed = []
    for i in range(blocks):
        here = jnp.zeros((1, LANES), jnp.int32)
        for j in range(lists_ref.shape[1]):
            block = lists_ref[i, j]
            here = jnp.where((block >= low) & (block < high), 1, here)
            inside = (block >= owner_low) & (block < owner_low + blocks)
            asked = jnp.maximum(asked, jnp.where(inside, block - owner_low + 1, 0))
        listed.append(here)
    note_out[0:blocks, :] = docs_ref[...]
    note_out[blocks : blocks + 1, :] = asked

    pl.semaphore_wait(barrier, seq_count + head_count + dp_count - 3)

    def note_copy(d):
        return pltpu.make_async_remote_copy(
            src_ref=note_out,
            dst_ref=note_in.at[d - 1],
            send_sem=note_ssem.at[d - 1],
            recv_sem=note_rsem.at[d - 1],
            device_id={"seq": lax.rem(own + d, seq_count)},
            device_id_type=MESH,
        )

    def kv_copy(d, h):
        return pltpu.make_async_remote_copy(
            src_ref=stage.at[d - 1, h],
            dst_ref=land.at[d - 1, h],
            send_sem=kv_ssem.at[d - 1, h],
            recv_sem=kv_rsem.at[d - 1, h],
            device_id={"seq": lax.rem(own + d, seq_count)},
            device_id_type=MESH,
        )

    def step_of(n):
        near = n // 2 + 1
        return jnp.where(lax.rem(n, 2) == 0, near, seq_count - near)

    for d in range(1, seq_count):
        note_copy(d).start()
    loads[0].wait()
    loads[1].wait()

    def fill(n, carry):
        d = step_of(n)
        note_copy(seq_count - d).wait_recv()
        row = note_in[seq_count - d - 1, blocks : blocks + 1, :]
        want = jnp.max(jnp.where(lane == own, row, 0), axis=1, keepdims=True)
        want = jnp.broadcast_to(jnp.maximum(want - 1, 0), (BLOCK, LANES))
        hots = [jnp.where(want == b, 1.0, 0.0).astype(jnp.bfloat16) for b in range(blocks)]
        for h in range(kv_heads):
            cut = slice(h * HEAD_SIZE, (h + 1) * HEAD_SIZE)
            for part, ref in enumerate((k_ref, v_ref)):
                picked = None
                for b in range(blocks):
                    term = ref[b * BLOCK : (b + 1) * BLOCK, cut] * hots[b]
                    picked = term if picked is None else picked + term
                stage[d - 1, h, part * BLOCK : (part + 1) * BLOCK, :] = picked
        return carry

    lax.fori_loop(0, seq_count - 1, fill, 0)

    @pl.when(core > 0)
    def _():
        pl.semaphore_wait(turn_sem, 1)

    def send_head(h, carry):
        def send(n, inner):
            kv_copy(step_of(n), h).start()
            return inner

        return lax.fori_loop(0, seq_count - 1, send, carry)

    lax.fori_loop(0, kv_heads, send_head, 0)

    lanes = lax.broadcasted_iota(jnp.int32, (BLOCK, LANES), 1)
    lanes_f = lanes.astype(jnp.float32)
    is_doc = lanes < DOCS

    def put_kext(s, row):
        same = jnp.where(column_of(row) == lanes_f, 1.0, 0.0)
        hot = jnp.where(is_doc, same, jnp.where(lanes == DOCS + s, 1.0, 0.0))
        at = s * BLOCK
        if not isinstance(s, int):
            at = pl.multiple_of(at, BLOCK)
        kext[pl.ds(at, BLOCK), :] = hot.astype(jnp.bfloat16)

    for i in range(blocks):
        row = docs_ref[i : i + 1, :]
        put_kext(i, row)
        same = jnp.where(column_of(row) == lanes_f, 0.0, -far_score)
        names = jnp.where(listed[i] > 0, 0.0, -far_score)
        qext[i] = jnp.where(is_doc, same, names).astype(jnp.bfloat16)

    def far_kext(d, carry):
        src = lax.rem(own - d + seq_count, seq_count)
        want = jnp.max(jnp.where(lane == src, asked, 0), axis=1, keepdims=True)
        want = jnp.maximum(want - 1, 0)
        note = note_in[d - 1]
        rows = lax.broadcasted_iota(jnp.int32, note.shape, 0)
        row = jnp.max(jnp.where(rows == want, note, 0), axis=0, keepdims=True)
        put_kext(blocks + d - 1, row)
        return carry

    lax.fori_loop(1, seq_count, far_kext, 0)
    loads[2].wait()

    ones = jnp.ones((BLOCK, LANES), jnp.bfloat16)

    def key_tile(s, h, which):
        if s < blocks:
            ref = v_ref if which else k_ref
            at = h * HEAD_SIZE
            if not isinstance(h, int):
                at = pl.multiple_of(at, HEAD_SIZE)
            return ref[s * BLOCK : (s + 1) * BLOCK, pl.ds(at, HEAD_SIZE)]
        return land[s - blocks, h, which * BLOCK : (which + 1) * BLOCK, :]

    chunks = [list(range(s, min(s + 2, slots))) for s in range(0, slots, 2)]
    parts = 2
    per = GROUP // parts

    def attend(h, i):
        at = pl.multiple_of(i * BLOCK, BLOCK)
        bias = qext[i]
        keys = [
            jnp.concatenate(
                [
                    jnp.concatenate(
                        [key_tile(s, h, 0), kext[s * BLOCK : (s + 1) * BLOCK, :]], axis=1
                    )
                    for s in chunk
                ],
                axis=0,
            )
            for chunk in chunks
        ]
        tops = []
        for part in range(parts):
            q = jnp.concatenate(
                [
                    jnp.concatenate(
                        [
                            q_ref[
                                pl.ds(at, BLOCK),
                                pl.ds(
                                    pl.multiple_of(
                                        h * width + (part * per + g) * HEAD_SIZE, HEAD_SIZE
                                    ),
                                    HEAD_SIZE,
                                ),
                            ],
                            bias,
                        ],
                        axis=1,
                    )
                    for g in range(per)
                ],
                axis=0,
            )
            top = None
            for chunk, k in zip(chunks, keys):
                s = lax.dot_general(
                    q, k, (((1,), (1,)), ((), ())), preferred_element_type=jnp.float32
                )
                for n, b in enumerate(chunk):
                    t = s[:, n * BLOCK : (n + 1) * BLOCK]
                    scores[part][:, b * BLOCK : (b + 1) * BLOCK] = t
                    top = t if top is None else jnp.maximum(top, t)
            tops.append(top)
        for part in range(parts):
            top = jnp.max(tops[part], axis=1, keepdims=True)
            for s in range(slots):
                here = slice(s * BLOCK, (s + 1) * BLOCK)
                probs[part][:, here] = jnp.exp2(
                    (scores[part][:, here] - top) * exp2_scale
                ).astype(jnp.bfloat16)
            v = jnp.concatenate(
                [jnp.concatenate([key_tile(s, h, 1), ones], axis=1) for s in range(slots)], axis=0
            )
            o = jnp.dot(probs[part][...], v, preferred_element_type=jnp.float32)
            o = (o[:, :HEAD_SIZE] / o[:, HEAD_SIZE:]).astype(jnp.bfloat16)
            for g in range(per):
                attn[
                    pl.ds(at, BLOCK),
                    pl.ds(
                        pl.multiple_of(h * width + (part * per + g) * HEAD_SIZE, HEAD_SIZE),
                        HEAD_SIZE,
                    ),
                ] = o[g * BLOCK : (g + 1) * BLOCK]

    def wait_head(h):
        def arrive(d, carry):
            kv_copy(d, h).wait_recv()
            return carry

        lax.fori_loop(1, seq_count, arrive, 0)

    def one_head(h, carry):
        wait_head(h)

        def one_row(i, inner):
            attend(h, i)
            return inner

        return lax.fori_loop(0, blocks, one_row, carry)

    lax.fori_loop(0, kv_heads - 1, one_head, 0)

    last = kv_heads - 1
    wait_head(last)

    def sent(n, carry):
        kv_copy(n // kv_heads + 1, lax.rem(n, kv_heads)).wait_send()
        return carry

    lax.fori_loop(0, (seq_count - 1) * kv_heads, sent, 0)

    @pl.when(core + 1 < dp_count)
    def _():
        pl.semaphore_signal(turn_sem, inc=1, device_id={"dp": core + 1}, device_id_type=MESH)

    loads[3].wait()

    def project(i, target, at, put):
        rows = attn[pl.ds(pl.multiple_of(i * BLOCK, BLOCK), BLOCK), :]
        for t in range(0, piece, tile):
            start = pl.multiple_of(target * cols + at + t, tile)
            put(
                t,
                jnp.dot(rows, w_ref[:, pl.ds(start, tile)], preferred_element_type=jnp.float32),
            )

    def y_copy(o, i, p):
        return pltpu.make_async_remote_copy(
            src_ref=ysend.at[o, i, p],
            dst_ref=yrecv.at[o, i, p],
            send_sem=y_ssem.at[o, i, p],
            recv_sem=y_rsem.at[o, i, p],
            device_id={"head": lax.rem(head + o + 1, head_count)},
            device_id_type=MESH,
        )

    per_row = others * PIECES

    def y_at(n):
        i = n // per_row
        rest = lax.rem(n, per_row)
        return rest // PIECES, i, lax.rem(rest, PIECES)

    def last_head(i, carry):
        attend(last, i)

        def share(n, inner):
            o, _, p = y_at(n)

            def put(t, x):
                ysend[o, i, p, :, t : t + tile] = x.astype(jnp.bfloat16)

            project(i, lax.rem(head + o + 1, head_count), p * piece, put)
            before = i * per_row + n - 1

            @pl.when(before >= 0)
            def _():
                y_copy(*y_at(before)).start()

            return inner

        return lax.fori_loop(0, per_row, share, carry)

    lax.fori_loop(0, blocks, last_head, 0)

    def own_share(n, carry):
        i = n // PIECES
        p = lax.rem(n, PIECES)
        rows = pl.ds(pl.multiple_of(i * BLOCK, BLOCK), BLOCK)

        def put(t, x):
            kept[rows, pl.ds(pl.multiple_of(p * piece + t, tile), tile)] = x

        project(i, head, p * piece, put)

        @pl.when(n == 0)
        def _():
            y_copy(*y_at(blocks * per_row - 1)).start()

        return carry

    lax.fori_loop(0, blocks * PIECES, own_share, 0)

    def out_copy(i):
        rows = pl.ds(pl.multiple_of(i * BLOCK, BLOCK), BLOCK)
        return pltpu.make_async_copy(done.at[rows, :], out_hbm.at[rows, :], out_sem.at[i])

    def finish(i, carry):
        rows = pl.ds(pl.multiple_of(i * BLOCK, BLOCK), BLOCK)
        for p in range(PIECES):
            total = kept[rows, p * piece : (p + 1) * piece]
            for o in range(others):
                y_copy(o, i, p).wait_recv()
                total = total + yrecv[o, i, p].astype(jnp.float32)
            done[rows, p * piece : (p + 1) * piece] = total.astype(jnp.bfloat16)
        out_copy(i).start()
        return carry

    lax.fori_loop(0, blocks, finish, 0)

    def drain(i, carry):
        for o in range(others):
            for p in range(PIECES):
                y_copy(o, i, p).wait_send()
        out_copy(i).wait()
        return carry

    lax.fori_loop(0, blocks, drain, 0)
    for d in range(1, seq_count):
        note_copy(d).wait_send()


def per_device(queries, keys, values, doc_ids, block_lists, w_out):
    tokens, depth = queries.shape
    blocks = tokens // BLOCK
    kv_width = keys.shape[1]
    kv_heads = kv_width // HEAD_SIZE
    seq_count = lax.axis_size("seq")
    head_count = lax.axis_size("head")
    dp_count = lax.axis_size("dp")
    far = seq_count - 1
    others = head_count - 1
    slots = blocks + far
    cols = w_out.shape[1] // head_count
    note_rows = -(-(blocks + 1) // 8) * 8
    assert DOCS + slots <= LANES
    hbm = pl.BlockSpec(memory_space=pl.ANY)
    bf16, f32, i32 = jnp.bfloat16, jnp.float32, jnp.int32
    half = GROUP // 2 * BLOCK
    return pl.pallas_call(
        functools.partial(kernel, seq_count, head_count, dp_count),
        out_shape=jax.ShapeDtypeStruct((tokens, cols), bf16),
        in_specs=[
            pl.BlockSpec(memory_space=pltpu.SMEM),
            pl.BlockSpec(memory_space=pltpu.VMEM),
            hbm,
            hbm,
            hbm,
            hbm,
        ],
        out_specs=hbm,
        scratch_shapes=[
            pltpu.VMEM((tokens, depth), bf16),
            pltpu.VMEM((tokens, kv_width), bf16),
            pltpu.VMEM((tokens, kv_width), bf16),
            pltpu.VMEM(w_out.shape, bf16),
            pltpu.VMEM((note_rows, LANES), i32),
            pltpu.VMEM((far, note_rows, LANES), i32),
            pltpu.VMEM((far, kv_heads, 2 * BLOCK, HEAD_SIZE), bf16),
            pltpu.VMEM((far, kv_heads, 2 * BLOCK, HEAD_SIZE), bf16),
            pltpu.VMEM((blocks, BLOCK, LANES), bf16),
            pltpu.VMEM((slots * BLOCK, LANES), bf16),
            [pltpu.VMEM((half, slots * BLOCK), f32) for _ in range(2)],
            [pltpu.VMEM((half, slots * BLOCK), bf16) for _ in range(2)],
            pltpu.VMEM((tokens, depth), bf16),
            pltpu.VMEM((others, blocks, PIECES, BLOCK, cols // PIECES), bf16),
            pltpu.VMEM((others, blocks, PIECES, BLOCK, cols // PIECES), bf16),
            pltpu.VMEM((tokens, cols), f32),
            pltpu.VMEM((tokens, cols), bf16),
            pltpu.SemaphoreType.DMA((4,)),
            pltpu.SemaphoreType.DMA((far,)),
            pltpu.SemaphoreType.DMA((far,)),
            pltpu.SemaphoreType.DMA((far, kv_heads)),
            pltpu.SemaphoreType.DMA((far, kv_heads)),
            pltpu.SemaphoreType.DMA((others, blocks, PIECES)),
            pltpu.SemaphoreType.DMA((others, blocks, PIECES)),
            pltpu.SemaphoreType.DMA((blocks,)),
            pltpu.SemaphoreType.REGULAR,
        ],
        compiler_params=pltpu.CompilerParams(
            collective_id=0, has_side_effects=True, vmem_limit_bytes=62 * 2**20
        ),
    )(block_lists, doc_ids.reshape(blocks, BLOCK), queries, keys, values, w_out)


def solution(mesh):
    in_specs = (
        P(("dp", "seq"), "head"),
        P(("dp", "seq"), "head"),
        P(("dp", "seq"), "head"),
        P(("dp", "seq")),
        P(("dp", "seq"), None),
        P("head", None),
    )
    out_specs = P(("dp", "seq"), "head")
    return jax.shard_map(
        per_device, mesh=mesh, in_specs=in_specs, out_specs=out_specs, check_vma=False
    )
```

profile of v0, /device:TPU:1, one launch (start us, length us, event | category | flops | bytes accessed | tf_op | source)
XLA Modules:
  0.0 99.4 jit_solution(11053578099788110379)
XLA Ops:
  0.0 96.3 %shard_map.64 = bf16[512,2048]{1,0:T(8,128)(2,1)} custom-call(s32[4,16]{1,0:T(4,128)} %lists_ref.1, s32[4,128]{1,0:T(4,128)} %bitcast.1, bf16[512,2048]{1,0:T(8,128)(2,1)} %q_hbm.1, bf16[512,512]{1,0:T(8,128)(2,1)} %k_hbm.1, bf16[512,512]{1,0:T(8,128)(2,1)} %v_hbm.1, bf16[2048,4096]{1,0:T(8,128)(2,1)} %w_hbm.1), custom_call_target="tpu_custom_call" | custom-call | tf_op jit(solution)/shard_map/pallas_call | solution.py:447
  96.3 3.2 %copy.8 = bf16[512,2048]{1,0:T(8,128)(2,1)} copy(bf16[512,2048]{1,0:T(8,128)(2,1)} %shard_map.64) | data formatting | bytes 4194304
where the time goes:
time: 100 us; the launch traced here: 99.4 us
  Pallas kernels  96.3 us (96%)
  local copies, waits for them, and re-layouts  3.16 us (3%)
    pallas_call x1, Pallas kernels, per_device(): pl.pallas_call(functools.partial(kernel, seq_count, head_count, dp_count)...  96.3 us
    unnamed x1, local copies, waits for them, and re-layouts  3.16 us

commit v1 on v0

v1 whole, which is shorter than its diff:
```python
import functools
import math

import jax
import jax.numpy as jnp
from jax import lax
from jax.experimental import pallas as pl
from jax.experimental.pallas import tpu as pltpu
from jax.sharding import PartitionSpec as P

HEAD_SIZE = 128
BLOCK = 128
LANES = 128
DOCS = 8
GROUP = 4
PIECES = 4
TILE = 512
MESH = pl.DeviceIdType.MESH

far_score = float(2**20)
exp2_scale = math.log2(math.e) / math.sqrt(HEAD_SIZE)


def column_of(row):
    return jnp.broadcast_to(row, (BLOCK, LANES)).astype(jnp.float32).T


def kernel(
    seq_count,
    head_count,
    dp_count,
    lists_hbm,
    docs_hbm,
    q_hbm,
    k_hbm,
    v_hbm,
    w_hbm,
    out_ref,
    lists_ref,
    docs_ref,
    q_ref,
    k_ref,
    v_ref,
    w_ref,
    note_out,
    note_in,
    stage,
    land,
    qext,
    kext,
    scores,
    probs,
    attn,
    ysend,
    yrecv,
    kept,
    own_sum,
    own_top,
    load_sem,
    note_ssem,
    note_rsem,
    kv_ssem,
    kv_rsem,
    y_ssem,
    y_rsem,
    turn_sem,
):
    own = lax.axis_index("seq")
    head = lax.axis_index("head")
    core = lax.axis_index("dp")
    blocks = docs_ref.shape[0]
    slots = blocks + seq_count - 1
    kv_heads = k_ref.shape[1] // HEAD_SIZE
    width = GROUP * HEAD_SIZE
    cols = kept.shape[1]
    piece = cols // PIECES
    tile = min(TILE, piece)
    others = head_count - 1

    loads = [
        pltpu.make_async_copy(src, dst, load_sem.at[n])
        for n, (src, dst) in enumerate(
            (
                (docs_hbm, docs_ref),
                (lists_hbm, lists_ref),
                (k_hbm, k_ref),
                (v_hbm, v_ref),
                (q_hbm, q_ref),
                (w_hbm, w_ref),
            )
        )
    ]
    for load in loads:
        load.start()

    barrier = pltpu.get_barrier_semaphore()
    for d in range(1, seq_count):
        pl.semaphore_signal(
            barrier, inc=1, device_id={"seq": lax.rem(own + d, seq_count)}, device_id_type=MESH
        )
    for d in range(1, head_count):
        pl.semaphore_signal(
            barrier, inc=1, device_id={"head": lax.rem(head + d, head_count)}, device_id_type=MESH
        )
    for d in range(1, dp_count):
        pl.semaphore_signal(
            barrier, inc=1, device_id={"dp": lax.rem(core + d, dp_count)}, device_id_type=MESH
        )

    loads[0].wait()
    loads[1].wait()

    lane = lax.broadcasted_iota(jnp.int32, (1, LANES), 1)
    slot = lane - DOCS
    source = own - (slot - blocks + 1)
    source = jnp.where(source < 0, source + seq_count, source)
    is_own = (slot >= 0) & (slot < blocks)
    is_far = (slot >= blocks) & (slot < slots)
    low = jnp.where(is_own, own * blocks + slot, jnp.where(is_far, source * blocks, -1))
    high = jnp.where(is_own, low + 1, jnp.where(is_far, low + blocks, -1))
    owner_low = lane * blocks
    asked = jnp.zeros((1, LANES), jnp.int32)
    listed = []
    for i in range(blocks):
        here = jnp.zeros((1, LANES), jnp.int32)
        for j in range(lists_ref.shape[1]):
            block = lists_ref[i, j]
            here = jnp.where((block >= low) & (block < high), 1, here)
            inside = (block >= owner_low) & (block < owner_low + blocks)
            asked = jnp.maximum(asked, jnp.where(inside, block - owner_low + 1, 0))
        listed.append(here)
    note_out[0:blocks, :] = docs_ref[...]
    note_out[blocks : blocks + 1, :] = asked

    pl.semaphore_wait(barrier, seq_count + head_count + dp_count - 3)

    def note_copy(d):
        return pltpu.make_async_remote_copy(
            src_ref=note_out,
            dst_ref=note_in.at[d - 1],
            send_sem=note_ssem.at[d - 1],
            recv_sem=note_rsem.at[d - 1],
            device_id={"seq": lax.rem(own + d, seq_count)},
            device_id_type=MESH,
        )

    def kv_copy(d, h):
        return pltpu.make_async_remote_copy(
            src_ref=stage.at[d - 1, h],
            dst_ref=land.at[d - 1, h],
            send_sem=kv_ssem.at[d - 1, h],
            recv_sem=kv_rsem.at[d - 1, h],
            device_id={"seq": lax.rem(own + d, seq_count)},
            device_id_type=MESH,
        )

    def step_of(n):
        near = n // 2 + 1
        return jnp.where(lax.rem(n, 2) == 0, near, seq_count - near)

    for d in range(1, seq_count):
        note_copy(d).start()
    loads[2].wait()
    loads[3].wait()
    loads[4].wait()

    def send_heads(first):
        def send_head(h, carry):
            def send(n, inner):
                kv_copy(step_of(n), h).start()
                return inner

            return lax.fori_loop(0, seq_count - 1, send, carry)

        lax.fori_loop(first, kv_heads, send_head, 0)

    lanes = lax.broadcasted_iota(jnp.int32, (BLOCK, LANES), 1)
    lanes_f = lanes.astype(jnp.float32)
    is_doc = lanes < DOCS

    def put_kext(s, row):
        same = jnp.where(column_of(row) == lanes_f, 1.0, 0.0)
        hot = jnp.where(is_doc, same, jnp.where(lanes == DOCS + s, 1.0, 0.0))
        at = s * BLOCK
        if not isinstance(s, int):
            at = pl.multiple_of(at, BLOCK)
        kext[pl.ds(at, BLOCK), :] = hot.astype(jnp.bfloat16)

    for i in range(blocks):
        row = docs_ref[i : i + 1, :]
        put_kext(i, row)
        same = jnp.where(column_of(row) == lanes_f, 0.0, -far_score)
        names = jnp.where(listed[i] > 0, 0.0, -far_score)
        qext[i] = jnp.where(is_doc, same, names).astype(jnp.bfloat16)

    def far_kext():
        for d in range(1, seq_count):
            src = lax.rem(own - d + seq_count, seq_count)
            want = jnp.max(jnp.where(lane == src, asked, 0), axis=1, keepdims=True)
            want = jnp.maximum(want - 1, 0)
            note = note_in[d - 1]
            rows = lax.broadcasted_iota(jnp.int32, note.shape, 0)
            row = jnp.max(jnp.where(rows == want, note, 0), axis=0, keepdims=True)
            put_kext(blocks + d - 1, row)

    ones = jnp.ones((BLOCK, LANES), jnp.bfloat16)

    def key_tile(s, h, which):
        if s < blocks:
            ref = v_ref if which else k_ref
            at = h * HEAD_SIZE
            if not isinstance(h, int):
                at = pl.multiple_of(at, HEAD_SIZE)
            return ref[s * BLOCK : (s + 1) * BLOCK, pl.ds(at, HEAD_SIZE)]
        return land[s - blocks, h, which * BLOCK : (which + 1) * BLOCK, :]

    parts = 2
    per = GROUP // parts
    part_rows = per * BLOCK

    def softmax_sums(h, i, names):
        at = pl.multiple_of(i * BLOCK, BLOCK)
        bias = qext[i]
        chunks = [names[n : n + 2] for n in range(0, len(names), 2)]
        keys = [
            jnp.concatenate(
                [
                    jnp.concatenate(
                        [key_tile(s, h, 0), kext[s * BLOCK : (s + 1) * BLOCK, :]], axis=1
                    )
                    for s in chunk
                ],
                axis=0,
            )
            for chunk in chunks
        ]
        v = jnp.concatenate(
            [jnp.concatenate([key_tile(s, h, 1), ones], axis=1) for s in names], axis=0
        )
        tops = []
        for part in range(parts):
            q = jnp.concatenate(
                [
                    jnp.concatenate([q_ref[pl.ds(at, BLOCK), head_cols(h, part * per + g)], bias], axis=1)
                    for g in range(per)
                ],
                axis=0,
            )
            top = None
            n = 0
            for k in keys:
                s = lax.dot_general(
                    q, k, (((1,), (1,)), ((), ())), preferred_element_type=jnp.float32
                )
                for m in range(k.shape[0] // BLOCK):
                    t = s[:, m * BLOCK : (m + 1) * BLOCK]
                    scores[part][:, n * BLOCK : (n + 1) * BLOCK] = t
                    top = t if top is None else jnp.maximum(top, t)
                    n += 1
            tops.append(top)
        found = []
        for part in range(parts):
            top = jnp.max(tops[part], axis=1, keepdims=True)
            for n in range(len(names)):
                here = slice(n * BLOCK, (n + 1) * BLOCK)
                probs[part][:, here] = jnp.exp2(
                    (scores[part][:, here] - top) * exp2_scale
                ).astype(jnp.bfloat16)
            o = jnp.dot(
                probs[part][:, : len(names) * BLOCK], v, preferred_element_type=jnp.float32
            )
            found.append((top, o))
        return found

    def head_cols(h, g):
        return pl.ds(pl.multiple_of(h * width + g * HEAD_SIZE, HEAD_SIZE), HEAD_SIZE)

    own_slots = list(range(blocks))
    far_slots = list(range(blocks, slots))

    def attend_own(n, carry):
        found = softmax_sums(n // blocks, lax.rem(n, blocks), own_slots)
        for part, (top, o) in enumerate(found):
            own_top[n, part] = jnp.broadcast_to(top, (part_rows, LANES))
            own_sum[n, part] = o
        return carry

    def attend(h, i):
        at = pl.multiple_of(i * BLOCK, BLOCK)
        n = h * blocks + i
        for part, (top, o) in enumerate(softmax_sums(h, i, far_slots)):
            first = own_top[n, part]
            both = jnp.maximum(first, top)
            near = jnp.exp2((first - both) * exp2_scale)
            far = jnp.exp2((top - both) * exp2_scale)
            x = own_sum[n, part]
            total = x[:, :HEAD_SIZE] * near + o[:, :HEAD_SIZE] * far
            count = x[:, HEAD_SIZE:] * near + o[:, HEAD_SIZE:] * far
            result = (total / count).astype(jnp.bfloat16)
            for g in range(per):
                attn[pl.ds(at, BLOCK), head_cols(h, part * per + g)] = result[
                    g * BLOCK : (g + 1) * BLOCK
                ]

    def fill(n, carry):
        d = step_of(n)
        note_copy(seq_count - d).wait_recv()
        row = note_in[seq_count - d - 1, blocks : blocks + 1, :]
        want = jnp.max(jnp.where(lane == own, row, 0), axis=1, keepdims=True)
        want = jnp.broadcast_to(jnp.maximum(want - 1, 0), (BLOCK, LANES))
        hots = [jnp.where(want == b, 1.0, 0.0).astype(jnp.bfloat16) for b in range(blocks)]
        for h in range(kv_heads):
            cut = slice(h * HEAD_SIZE, (h + 1) * HEAD_SIZE)
            for part, ref in enumerate((k_ref, v_ref)):
                picked = None
                for b in range(blocks):
                    term = ref[b * BLOCK : (b + 1) * BLOCK, cut] * hots[b]
                    picked = term if picked is None else picked + term
                stage[d - 1, h, part * BLOCK : (part + 1) * BLOCK, :] = picked

        @pl.when(core == 0)
        def _():
            for h in range(early):
                kv_copy(d, h).start()

        @pl.when(n < kv_heads * blocks)
        def _():
            attend_own(n, 0)

        return carry

    early = min(2, kv_heads)
    lax.fori_loop(0, seq_count - 1, fill, 0)

    @pl.when(core == 0)
    def _():
        send_heads(early)

    lax.fori_loop(min(seq_count - 1, kv_heads * blocks), kv_heads * blocks, attend_own, 0)

    @pl.when(core > 0)
    def _():
        pl.semaphore_wait(turn_sem, 1)
        send_heads(0)

    far_kext()

    def wait_head(h):
        def arrive(d, carry):
            kv_copy(d, h).wait_recv()
            return carry

        lax.fori_loop(1, seq_count, arrive, 0)

    def one_head(h, carry):
        wait_head(h)

        def one_row(i, inner):
            attend(h, i)
            return inner

        return lax.fori_loop(0, blocks, one_row, carry)

    lax.fori_loop(0, kv_heads - 1, one_head, 0)

    @pl.when(core + 1 < dp_count)
    def _():
        pl.semaphore_signal(turn_sem, inc=1, device_id={"dp": core + 1}, device_id_type=MESH)

    last = kv_heads - 1
    wait_head(last)
    loads[5].wait()

    def project(i, target, at, put):
        rows = attn[pl.ds(pl.multiple_of(i * BLOCK, BLOCK), BLOCK), :]
        for t in range(0, piece, tile):
            start = pl.multiple_of(target * cols + at + t, tile)
            put(
                t,
                jnp.dot(rows, w_ref[:, pl.ds(start, tile)], preferred_element_type=jnp.float32),
            )

    def y_copy(o, i, p):
        return pltpu.make_async_remote_copy(
            src_ref=ysend.at[o, i, p],
            dst_ref=yrecv.at[o, i, p],
            send_sem=y_ssem.at[o, i, p],
            recv_sem=y_rsem.at[o, i, p],
            device_id={"head": lax.rem(head + o + 1, head_count)},
            device_id_type=MESH,
        )

    per_row = others * PIECES

    def y_at(n):
        i = n // per_row
        rest = lax.rem(n, per_row)
        return rest // PIECES, i, lax.rem(rest, PIECES)

    def last_head(i, carry):
        attend(last, i)

        def share(n, inner):
            o, _, p = y_at(n)

            def put(t, x):
                ysend[o, i, p, :, t : t + tile] = x.astype(jnp.bfloat16)

            project(i, lax.rem(head + o + 1, head_count), p * piece, put)
            before = i * per_row + n - 1

            @pl.when(before >= 0)
            def _():
                y_copy(*y_at(before)).start()

            return inner

        return lax.fori_loop(0, per_row, share, carry)

    lax.fori_loop(0, blocks, last_head, 0)

    def own_share(n, carry):
        i = n // PIECES
        p = lax.rem(n, PIECES)
        rows = pl.ds(pl.multiple_of(i * BLOCK, BLOCK), BLOCK)

        def put(t, x):
            kept[rows, pl.ds(pl.multiple_of(p * piece + t, tile), tile)] = x

        project(i, head, p * piece, put)

        @pl.when(n == 0)
        def _():
            y_copy(*y_at(blocks * per_row - 1)).start()

        return carry

    lax.fori_loop(0, blocks * PIECES, own_share, 0)

    for d in range(1, seq_count):
        note_copy(d).wait_send()

    def sent(n, carry):
        kv_copy(n // kv_heads + 1, lax.rem(n, kv_heads)).wait_send()
        return carry

    lax.fori_loop(0, (seq_count - 1) * kv_heads, sent, 0)

    def finish(i, carry):
        rows = pl.ds(pl.multiple_of(i * BLOCK, BLOCK), BLOCK)
        for p in range(PIECES):
            total = kept[rows, p * piece : (p + 1) * piece]
            for o in range(others):
                y_copy(o, i, p).wait_recv()
                total = total + yrecv[o, i, p].astype(jnp.float32)
            out_ref[rows, p * piece : (p + 1) * piece] = total.astype(jnp.bfloat16)
            for o in range(others):
                y_copy(o, i, p).wait_send()
        return carry

    lax.fori_loop(0, blocks, finish, 0)


def per_device(queries, keys, values, doc_ids, block_lists, w_out):
    tokens, depth = queries.shape
    blocks = tokens // BLOCK
    kv_width = keys.shape[1]
    kv_heads = kv_width // HEAD_SIZE
    seq_count = lax.axis_size("seq")
    head_count = lax.axis_size("head")
    dp_count = lax.axis_size("dp")
    far = seq_count - 1
    others = head_count - 1
    slots = blocks + far
    cols = w_out.shape[1] // head_count
    note_rows = -(-(blocks + 1) // 8) * 8
    assert DOCS + slots <= LANES
    hbm = pl.BlockSpec(memory_space=pl.ANY)
    bf16, f32, i32 = jnp.bfloat16, jnp.float32, jnp.int32
    half = GROUP // 2 * BLOCK
    return pl.pallas_call(
        functools.partial(kernel, seq_count, head_count, dp_count),
        out_shape=jax.ShapeDtypeStruct((tokens, cols), bf16),
        in_specs=[
            hbm,
        ]
        * 6,
        out_specs=pl.BlockSpec(memory_space=pltpu.VMEM),
        scratch_shapes=[
            pltpu.SMEM(block_lists.shape, i32),
            pltpu.VMEM((blocks, BLOCK), i32),
            pltpu.VMEM((tokens, depth), bf16),
            pltpu.VMEM((tokens, kv_width), bf16),
            pltpu.VMEM((tokens, kv_width), bf16),
            pltpu.VMEM(w_out.shape, bf16),
            pltpu.VMEM((note_rows, LANES), i32),
            pltpu.VMEM((far, note_rows, LANES), i32),
            pltpu.VMEM((far, kv_heads, 2 * BLOCK, HEAD_SIZE), bf16),
            pltpu.VMEM((far, kv_heads, 2 * BLOCK, HEAD_SIZE), bf16),
            pltpu.VMEM((blocks, BLOCK, LANES), bf16),
            pltpu.VMEM((slots * BLOCK, LANES), bf16),
            [pltpu.VMEM((half, max(blocks, far) * BLOCK), f32) for _ in range(2)],
            [pltpu.VMEM((half, max(blocks, far) * BLOCK), bf16) for _ in range(2)],
            pltpu.VMEM((tokens, depth), bf16),
            pltpu.VMEM((others, blocks, PIECES, BLOCK, cols // PIECES), bf16),
            pltpu.VMEM((others, blocks, PIECES, BLOCK, cols // PIECES), bf16),
            pltpu.VMEM((tokens, cols), f32),
            pltpu.VMEM((kv_heads * blocks, 2, half, 2 * LANES), f32),
            pltpu.VMEM((kv_heads * blocks, 2, half, LANES), f32),
            pltpu.SemaphoreType.DMA((6,)),
            pltpu.SemaphoreType.DMA((far,)),
            pltpu.SemaphoreType.DMA((far,)),
            pltpu.SemaphoreType.DMA((far, kv_heads)),
            pltpu.SemaphoreType.DMA((far, kv_heads)),
            pltpu.SemaphoreType.DMA((others, blocks, PIECES)),
            pltpu.SemaphoreType.DMA((others, blocks, PIECES)),
            pltpu.SemaphoreType.REGULAR,
        ],
        compiler_params=pltpu.CompilerParams(
            collective_id=0, has_side_effects=True, vmem_limit_bytes=51500 * 2**10
        ),
    )(
        *[
            pltpu.with_memory_space_constraint(x, pltpu.HBM)
            for x in (
                block_lists,
                doc_ids.reshape(blocks, BLOCK),
                queries,
                keys,
                values,
                w_out,
            )
        ]
    )


def solution(mesh):
    in_specs = (
        P(("dp", "seq"), "head"),
        P(("dp", "seq"), "head"),
        P(("dp", "seq"), "head"),
        P(("dp", "seq")),
        P(("dp", "seq"), None),
        P("head", None),
    )
    out_specs = P(("dp", "seq"), "head")
    return jax.shard_map(
        per_device, mesh=mesh, in_specs=in_specs, out_specs=out_specs, check_vma=False
    )
```

time: 100 us -> 90.7 us (0.907)
  Pallas kernels: 96.3 us -> 89.2 us
  local copies, waits for them, and re-layouts: 3.16 us -> 1.32 us
    pallas_call x1, Pallas kernels: 96.3 us -> 89.2 us  [per_device(): pl.pallas_call(functools.partial(kernel, seq_count, head_count, dp_count)...]
    unnamed x1, local copies, waits for them, and re-layouts: 3.16 us -> 1.32 us
where the time goes in v1:
time: 90.7 us; the launch traced here: 90.6 us
  Pallas kernels  89.2 us (98%)
  local copies, waits for them, and re-layouts  1.32 us (1%)
    pallas_call x1, Pallas kernels, per_device(): pl.pallas_call(functools.partial(kernel, seq_count, head_count, dp_count)...  89.2 us

profile of v1, /device:TPU:1, one launch (start us, length us, event | category | flops | bytes accessed | tf_op | source)
XLA Modules:
  0.0 90.6 jit_solution(5738368555315687410)
XLA Ops:
  0.0 89.2 %shard_map.64 = bf16[512,2048]{1,0:T(8,128)(2,1)S(1)} custom-call(s32[4,16]{1,0:T(4,128)} %lists_hbm.1, s32[4,128]{1,0:T(4,128)} %bitcast.1, bf16[512,2048]{1,0:T(8,128)(2,1)} %q_hbm.1, bf16[512,512]{1,0:T(8,128)(2,1)} %k_hbm.1, bf16[512,512]{1,0:T(8,128)(2,1)} %v_hbm.1, bf16[2048,4096]{1,0:T(8,128)(2,1)} %w_hbm.1), custom_call_target="tpu_custom_call" | custom-call | tf_op jit(solution)/shard_map/pallas_call | solution.py:481
  89.3 1.3 %copy.8 = bf16[512,2048]{1,0:T(8,128)(2,1)} copy(bf16[512,2048]{1,0:T(8,128)(2,1)S(1)} %shard_map.64) | data formatting | bytes 4194304

commit v2 on v1

--- a/solution.py
+++ b/solution.py
@@ -14,7 +14,7 @@
 DOCS = 8
 GROUP = 4
 PIECES = 4
-TILE = 512
+TILE = 1024
 MESH = pl.DeviceIdType.MESH
 
 far_score = float(2**20)
@@ -73,8 +73,10 @@
     kv_heads = k_ref.shape[1] // HEAD_SIZE
     width = GROUP * HEAD_SIZE
     cols = kept.shape[1]
-    piece = cols // PIECES
-    tile = min(TILE, piece)
+    pieces = ysend.shape[2]
+    piece = cols // pieces
+    tile = math.gcd(TILE, cols)
+    own_tiles = cols // tile
     others = head_count - 1
 
     loads = [
@@ -154,20 +156,24 @@
             device_id_type=MESH,
         )
 
+    sides = jnp.minimum(own, seq_count - 1 - own)
+
     def step_of(n):
-        near = n // 2 + 1
-        return jnp.where(lax.rem(n, 2) == 0, near, seq_count - near)
+        pair = n // 2 + 1
+        rest = n - sides + 1
+        both = jnp.where(lax.rem(n, 2) == 0, pair, seq_count - pair)
+        one = jnp.where(own < seq_count - 1 - own, rest, seq_count - rest)
+        return jnp.where(n < 2 * sides, both, one)
 
     for d in range(1, seq_count):
         note_copy(d).start()
     loads[2].wait()
     loads[3].wait()
-    loads[4].wait()
 
     def send_heads(first):
         def send_head(h, carry):
             def send(n, inner):
-                kv_copy(step_of(n), h).start()
+                kv_copy(step_of(seq_count - 2 - n), h).start()
                 return inner
 
             return lax.fori_loop(0, seq_count - 1, send, carry)
@@ -218,9 +224,7 @@
     per = GROUP // parts
     part_rows = per * BLOCK
 
-    def softmax_sums(h, i, names):
-        at = pl.multiple_of(i * BLOCK, BLOCK)
-        bias = qext[i]
+    def softmax_sums(h, rows, names, put):
         chunks = [names[n : n + 2] for n in range(0, len(names), 2)]
         keys = [
             jnp.concatenate(
@@ -237,11 +241,17 @@
         v = jnp.concatenate(
             [jnp.concatenate([key_tile(s, h, 1), ones], axis=1) for s in names], axis=0
         )
-        tops = []
-        for part in range(parts):
+        units = [(i, part) for i in rows for part in range(parts)]
+
+        def score(u):
+            i, part = units[u]
+            at = pl.multiple_of(i * BLOCK, BLOCK)
+            bias = qext[i]
             q = jnp.concatenate(
                 [
-                    jnp.concatenate([q_ref[pl.ds(at, BLOCK), head_cols(h, part * per + g)], bias], axis=1)
+                    jnp.concatenate(
+                        [q_ref[pl.ds(at, BLOCK), head_cols(h, part * per + g)], bias], axis=1
+                    )
                     for g in range(per)
                 ],
                 axis=0,
@@ -254,23 +264,25 @@
                 )
                 for m in range(k.shape[0] // BLOCK):
                     t = s[:, m * BLOCK : (m + 1) * BLOCK]
-                    scores[part][:, n * BLOCK : (n + 1) * BLOCK] = t
+                    scores[u % 2][:, n * BLOCK : (n + 1) * BLOCK] = t
                     top = t if top is None else jnp.maximum(top, t)
                     n += 1
-            tops.append(top)
-        found = []
-        for part in range(parts):
-            top = jnp.max(tops[part], axis=1, keepdims=True)
+            return top
+
+        top = score(0)
+        for u, (i, part) in enumerate(units):
+            later = score(u + 1) if u + 1 < len(units) else None
+            top = jnp.max(top, axis=1, keepdims=True)
             for n in range(len(names)):
                 here = slice(n * BLOCK, (n + 1) * BLOCK)
-                probs[part][:, here] = jnp.exp2(
-                    (scores[part][:, here] - top) * exp2_scale
+                probs[u % 2][:, here] = jnp.exp2(
+                    (scores[u % 2][:, here] - top) * exp2_scale
                 ).astype(jnp.bfloat16)
             o = jnp.dot(
-                probs[part][:, : len(names) * BLOCK], v, preferred_element_type=jnp.float32
+                probs[u % 2][:, : len(names) * BLOCK], v, preferred_element_type=jnp.float32
             )
-            found.append((top, o))
-        return found
+            put(i, part, top, o)
+            top = later
 
     def head_cols(h, g):
         return pl.ds(pl.multiple_of(h * width + g * HEAD_SIZE, HEAD_SIZE), HEAD_SIZE)
@@ -278,17 +290,26 @@
     own_slots = list(range(blocks))
     far_slots = list(range(blocks, slots))
 
+    span = math.gcd(blocks, 2)
+    steps = blocks // span
+
+    def rows_of(n):
+        return [n * span + r for r in range(span)]
+
     def attend_own(n, carry):
-        found = softmax_sums(n // blocks, lax.rem(n, blocks), own_slots)
-        for part, (top, o) in enumerate(found):
-            own_top[n, part] = jnp.broadcast_to(top, (part_rows, LANES))
-            own_sum[n, part] = o
+        h = n // steps
+
+        def put(i, part, top, o):
+            own_top[h * blocks + i, part] = jnp.broadcast_to(top, (part_rows, LANES))
+            own_sum[h * blocks + i, part] = o
+
+        softmax_sums(h, rows_of(lax.rem(n, steps)), own_slots, put)
         return carry
 
-    def attend(h, i):
-        at = pl.multiple_of(i * BLOCK, BLOCK)
-        n = h * blocks + i
-        for part, (top, o) in enumerate(softmax_sums(h, i, far_slots)):
+    def attend(h, rows):
+        def put(i, part, top, o):
+            at = pl.multiple_of(i * BLOCK, BLOCK)
+            n = h * blocks + i
             first = own_top[n, part]
             both = jnp.maximum(first, top)
             near = jnp.exp2((first - both) * exp2_scale)
@@ -301,6 +322,8 @@
                 attn[pl.ds(at, BLOCK), head_cols(h, part * per + g)] = result[
                     g * BLOCK : (g + 1) * BLOCK
                 ]
+
+        softmax_sums(h, rows, far_slots, put)
 
     def fill(n, carry):
         d = step_of(n)
@@ -320,23 +343,19 @@
 
         @pl.when(core == 0)
         def _():
-            for h in range(early):
-                kv_copy(d, h).start()
-
-        @pl.when(n < kv_heads * blocks)
-        def _():
-            attend_own(n, 0)
+            kv_copy(d, 0).start()
 
         return carry
 
-    early = min(2, kv_heads)
+    own_steps = kv_heads * steps
     lax.fori_loop(0, seq_count - 1, fill, 0)
 
     @pl.when(core == 0)
     def _():
-        send_heads(early)
-
-    lax.fori_loop(min(seq_count - 1, kv_heads * blocks), kv_heads * blocks, attend_own, 0)
+        send_heads(1)
+
+    loads[4].wait()
+    lax.fori_loop(0, own_steps, attend_own, 0)
 
     @pl.when(core > 0)
     def _():
@@ -356,29 +375,29 @@
         wait_head(h)
 
         def one_row(i, inner):
-            attend(h, i)
+            attend(h, rows_of(i))
             return inner
 
-        return lax.fori_loop(0, blocks, one_row, carry)
-
-    lax.fori_loop(0, kv_heads - 1, one_head, 0)
+        return lax.fori_loop(0, steps, one_row, carry)
+
+    last = kv_heads - 1
+    before_last = max(last - 1, 0)
+    lax.fori_loop(0, before_last, one_head, 0)
+    for h in range(before_last, last):
+        wait_head(h)
+        attend(h, [0])
 
     @pl.when(core + 1 < dp_count)
     def _():
         pl.semaphore_signal(turn_sem, inc=1, device_id={"dp": core + 1}, device_id_type=MESH)
 
-    last = kv_heads - 1
     wait_head(last)
     loads[5].wait()
 
-    def project(i, target, at, put):
+    def project(i, target, at, size, put):
         rows = attn[pl.ds(pl.multiple_of(i * BLOCK, BLOCK), BLOCK), :]
-        for t in range(0, piece, tile):
-            start = pl.multiple_of(target * cols + at + t, tile)
-            put(
-                t,
-                jnp.dot(rows, w_ref[:, pl.ds(start, tile)], preferred_element_type=jnp.float32),
-            )
+        start = pl.multiple_of(target * cols + at, size)
+        put(jnp.dot(rows, w_ref[:, pl.ds(start, size)], preferred_element_type=jnp.float32))
 
     def y_copy(o, i, p):
         return pltpu.make_async_remote_copy(
@@ -390,52 +409,68 @@
             device_id_type=MESH,
         )
 
-    per_row = others * PIECES
-
-    def y_at(n):
-        i = n // per_row
-        rest = lax.rem(n, per_row)
-        return rest // PIECES, i, lax.rem(rest, PIECES)
-
-    def last_head(i, carry):
-        attend(last, i)
-
-        def share(n, inner):
-            o, _, p = y_at(n)
-
-            def put(t, x):
-                ysend[o, i, p, :, t : t + tile] = x.astype(jnp.bfloat16)
-
-            project(i, lax.rem(head + o + 1, head_count), p * piece, put)
-            before = i * per_row + n - 1
-
-            @pl.when(before >= 0)
-            def _():
-                y_copy(*y_at(before)).start()
-
-            return inner
-
-        return lax.fori_loop(0, per_row, share, carry)
-
-    lax.fori_loop(0, blocks, last_head, 0)
+    def share(i, size):
+        groups = [
+            (o, range(p, min(p + size, pieces)))
+            for o in range(others)
+            for p in range(0, pieces, size)
+        ]
+        for n, (o, group) in enumerate(groups):
+            target = lax.rem(head + o + 1, head_count)
+
+            def put(x):
+                for p in group:
+                    at = (p - group[0]) * piece
+                    ysend[o, i, p] = x[:, at : at + piece].astype(jnp.bfloat16)
+
+            project(i, target, group[0] * piece, len(group) * piece, put)
+            if n > 0:
+                for p in groups[n - 1][1]:
+                    y_copy(groups[n - 1][0], i, p).start()
+        return groups[-1]
+
+    def send_rest(i, group):
+        for p in group[1]:
+            y_copy(group[0], i, p).start()
+
+    def tail_row(i, carry):
+        for h in range(before_last, last):
+            attend(h, [i])
+
+        @pl.when(i == 1)
+        def _():
+            send_rest(0, first_rest)
+
+        @pl.when(i > 1)
+        def _():
+            send_rest(i - 1, rest)
+
+        attend(last, [i])
+        share(i, 2)
+        return carry
+
+    attend(last, [0])
+    first_rest = share(0, 1)
+    rest = (others - 1, range((pieces - 1) // 2 * 2, pieces))
+    lax.fori_loop(1, blocks, tail_row, 0)
 
     def own_share(n, carry):
-        i = n // PIECES
-        p = lax.rem(n, PIECES)
+        i = n // own_tiles
+        at = pl.multiple_of(lax.rem(n, own_tiles) * tile, tile)
         rows = pl.ds(pl.multiple_of(i * BLOCK, BLOCK), BLOCK)
 
-        def put(t, x):
-            kept[rows, pl.ds(pl.multiple_of(p * piece + t, tile), tile)] = x
-
-        project(i, head, p * piece, put)
+        def put(x):
+            kept[rows, pl.ds(at, tile)] = x
+
+        project(i, head, at, tile, put)
 
         @pl.when(n == 0)
         def _():
-            y_copy(*y_at(blocks * per_row - 1)).start()
+            send_rest(blocks - 1, rest if blocks > 1 else first_rest)
 
         return carry
 
-    lax.fori_loop(0, blocks * PIECES, own_share, 0)
+    lax.fori_loop(0, blocks * own_tiles, own_share, 0)
 
     for d in range(1, seq_count):
         note_copy(d).wait_send()
@@ -448,7 +483,7 @@
 
     def finish(i, carry):
         rows = pl.ds(pl.multiple_of(i * BLOCK, BLOCK), BLOCK)
-        for p in range(PIECES):
+        for p in range(pieces):
             total = kept[rows, p * piece : (p + 1) * piece]
             for o in range(others):
                 y_copy(o, i, p).wait_recv()
@@ -473,6 +508,7 @@
     others = head_count - 1
     slots = blocks + far
     cols = w_out.shape[1] // head_count
+    pieces = math.gcd(PIECES, cols // LANES)
     note_rows = -(-(blocks + 1) // 8) * 8
     assert DOCS + slots <= LANES
     hbm = pl.BlockSpec(memory_space=pl.ANY)
@@ -502,8 +538,8 @@
             [pltpu.VMEM((half, max(blocks, far) * BLOCK), f32) for _ in range(2)],
             [pltpu.VMEM((half, max(blocks, far) * BLOCK), bf16) for _ in range(2)],
             pltpu.VMEM((tokens, depth), bf16),
-            pltpu.VMEM((others, blocks, PIECES, BLOCK, cols // PIECES), bf16),
-            pltpu.VMEM((others, blocks, PIECES, BLOCK, cols // PIECES), bf16),
+            pltpu.VMEM((others, blocks, pieces, BLOCK, cols // pieces), bf16),
+            pltpu.VMEM((others, blocks, pieces, BLOCK, cols // pieces), bf16),
             pltpu.VMEM((tokens, cols), f32),
             pltpu.VMEM((kv_heads * blocks, 2, half, 2 * LANES), f32),
             pltpu.VMEM((kv_heads * blocks, 2, half, LANES), f32),
@@ -512,8 +548,8 @@
             pltpu.SemaphoreType.DMA((far,)),
             pltpu.SemaphoreType.DMA((far, kv_heads)),
             pltpu.SemaphoreType.DMA((far, kv_heads)),
-            pltpu.SemaphoreType.DMA((others, blocks, PIECES)),
-            pltpu.SemaphoreType.DMA((others, blocks, PIECES)),
+            pltpu.SemaphoreType.DMA((others, blocks, pieces)),
+            pltpu.SemaphoreType.DMA((others, blocks, pieces)),
             pltpu.SemaphoreType.REGULAR,
         ],
         compiler_params=pltpu.CompilerParams(

time: 90.7 us -> 84.5 us (0.932)
  Pallas kernels: 89.2 us -> 83 us
    pallas_call x1, Pallas kernels: 89.2 us -> 83 us  [per_device(): pl.pallas_call(functools.partial(kernel, seq_count, head_count, dp_count)...]
where the time goes in v2:
time: 84.5 us; the launch traced here: 84.4 us
  Pallas kernels  83 us (98%)
  local copies, waits for them, and re-layouts  1.32 us (2%)
    pallas_call x1, Pallas kernels, per_device(): pl.pallas_call(functools.partial(kernel, seq_count, head_count, dp_count)...  83 us

profile of v2, /device:TPU:1, one launch (start us, length us, event | category | flops | bytes accessed | tf_op | source)
XLA Modules:
  0.0 84.4 jit_solution(13838027747195008728)
XLA Ops:
  0.0 83.0 %shard_map.64 = bf16[512,2048]{1,0:T(8,128)(2,1)S(1)} custom-call(s32[4,16]{1,0:T(4,128)} %lists_hbm.1, s32[4,128]{1,0:T(4,128)} %bitcast.1, bf16[512,2048]{1,0:T(8,128)(2,1)} %q_hbm.1, bf16[512,512]{1,0:T(8,128)(2,1)} %k_hbm.1, bf16[512,512]{1,0:T(8,128)(2,1)} %v_hbm.1, bf16[2048,4096]{1,0:T(8,128)(2,1)} %w_hbm.1), custom_call_target="tpu_custom_call" | custom-call | tf_op jit(solution)/shard_map/pallas_call | solution.py:517
  83.0 1.3 %copy.8 = bf16[512,2048]{1,0:T(8,128)(2,1)} copy(bf16[512,2048]{1,0:T(8,128)(2,1)S(1)} %shard_map.64) | data formatting | bytes 4194304

commit v3 on v2

--- a/solution.py
+++ b/solution.py
@@ -35,7 +35,7 @@
     k_hbm,
     v_hbm,
     w_hbm,
-    out_ref,
+    out_hbm,
     lists_ref,
     docs_ref,
     q_ref,
@@ -56,6 +56,7 @@
     kept,
     own_sum,
     own_top,
+    first_share,
     load_sem,
     note_ssem,
     note_rsem,
@@ -63,6 +64,7 @@
     kv_rsem,
     y_ssem,
     y_rsem,
+    out_sem,
     turn_sem,
 ):
     own = lax.axis_index("seq")
@@ -78,6 +80,8 @@
     tile = math.gcd(TILE, cols)
     own_tiles = cols // tile
     others = head_count - 1
+    last = kv_heads - 1
+    middle = 1 + (seq_count - 1) * 4 // 7
 
     loads = [
         pltpu.make_async_copy(src, dst, load_sem.at[n])
@@ -131,16 +135,21 @@
             inside = (block >= owner_low) & (block < owner_low + blocks)
             asked = jnp.maximum(asked, jnp.where(inside, block - owner_low + 1, 0))
         listed.append(here)
-    note_out[0:blocks, :] = docs_ref[...]
-    note_out[blocks : blocks + 1, :] = asked
+    for d in range(1, seq_count):
+        owner = lax.rem(own + d, seq_count)
+        want = jnp.max(jnp.where(lane == owner, asked, 0), axis=1, keepdims=True)
+        note_out[d - 1, 0:blocks, :] = docs_ref[...]
+        note_out[d - 1, blocks : blocks + 1, :] = jnp.broadcast_to(
+            jnp.maximum(want - 1, 0), (1, LANES)
+        )
 
     pl.semaphore_wait(barrier, seq_count + head_count + dp_count - 3)
 
     def note_copy(d):
         return pltpu.make_async_remote_copy(
-            src_ref=note_out,
+            src_ref=note_out.at[d - 1],
             dst_ref=note_in.at[d - 1],
-            send_sem=note_ssem.at[d - 1],
+            send_sem=note_ssem,
             recv_sem=note_rsem.at[d - 1],
             device_id={"seq": lax.rem(own + d, seq_count)},
             device_id_type=MESH,
@@ -150,11 +159,14 @@
         return pltpu.make_async_remote_copy(
             src_ref=stage.at[d - 1, h],
             dst_ref=land.at[d - 1, h],
-            send_sem=kv_ssem.at[d - 1, h],
-            recv_sem=kv_rsem.at[d - 1, h],
+            send_sem=kv_ssem,
+            recv_sem=kv_rsem.at[jnp.where((h == last) & (d >= middle), kv_heads, h)],
             device_id={"seq": lax.rem(own + d, seq_count)},
             device_id_type=MESH,
         )
+
+    def other(axis, at, count):
+        return {axis: lax.rem(at + 1, count)}
 
     sides = jnp.minimum(own, seq_count - 1 - own)
 
@@ -173,7 +185,7 @@
     def send_heads(first):
         def send_head(h, carry):
             def send(n, inner):
-                kv_copy(step_of(seq_count - 2 - n), h).start()
+                kv_copy(n + 1, h).start()
                 return inner
 
             return lax.fori_loop(0, seq_count - 1, send, carry)
@@ -201,9 +213,7 @@
 
     def far_kext():
         for d in range(1, seq_count):
-            src = lax.rem(own - d + seq_count, seq_count)
-            want = jnp.max(jnp.where(lane == src, asked, 0), axis=1, keepdims=True)
-            want = jnp.maximum(want - 1, 0)
+            want = note_out[seq_count - d - 1, blocks : blocks + 1, :]
             note = note_in[d - 1]
             rows = lax.broadcasted_iota(jnp.int32, note.shape, 0)
             row = jnp.max(jnp.where(rows == want, note, 0), axis=0, keepdims=True)
@@ -306,7 +316,7 @@
         softmax_sums(h, rows_of(lax.rem(n, steps)), own_slots, put)
         return carry
 
-    def attend(h, rows):
+    def attend(h, rows, names=far_slots, final=True):
         def put(i, part, top, o):
             at = pl.multiple_of(i * BLOCK, BLOCK)
             n = h * blocks + i
@@ -317,22 +327,24 @@
             x = own_sum[n, part]
             total = x[:, :HEAD_SIZE] * near + o[:, :HEAD_SIZE] * far
             count = x[:, HEAD_SIZE:] * near + o[:, HEAD_SIZE:] * far
+            if not final:
+                own_top[n, part] = both
+                own_sum[n, part, :, :HEAD_SIZE] = total
+                own_sum[n, part, :, HEAD_SIZE:] = count
+                return
             result = (total / count).astype(jnp.bfloat16)
             for g in range(per):
                 attn[pl.ds(at, BLOCK), head_cols(h, part * per + g)] = result[
                     g * BLOCK : (g + 1) * BLOCK
                 ]
 
-        softmax_sums(h, rows, far_slots, put)
-
-    def fill(n, carry):
-        d = step_of(n)
-        note_copy(seq_count - d).wait_recv()
-        row = note_in[seq_count - d - 1, blocks : blocks + 1, :]
-        want = jnp.max(jnp.where(lane == own, row, 0), axis=1, keepdims=True)
-        want = jnp.broadcast_to(jnp.maximum(want - 1, 0), (BLOCK, LANES))
+        softmax_sums(h, rows, names, put)
+
+    def pick(d, heads):
+        want = note_in[seq_count - d - 1, blocks : blocks + 1, :]
+        want = jnp.broadcast_to(want, (BLOCK, LANES))
         hots = [jnp.where(want == b, 1.0, 0.0).astype(jnp.bfloat16) for b in range(blocks)]
-        for h in range(kv_heads):
+        for h in heads:
             cut = slice(h * HEAD_SIZE, (h + 1) * HEAD_SIZE)
             for part, ref in enumerate((k_ref, v_ref)):
                 picked = None
@@ -341,14 +353,30 @@
                     picked = term if picked is None else picked + term
                 stage[d - 1, h, part * BLOCK : (part + 1) * BLOCK, :] = picked
 
-        @pl.when(core == 0)
+    def fill_first(n, carry):
+        d = step_of(n)
+        note_copy(seq_count - d).wait_recv()
+        pick(d, [0])
+
+        @pl.when((core == 0) & (n > 0))
         def _():
-            kv_copy(d, 0).start()
+            kv_copy(step_of(n - 1), 0).start()
 
         return carry
 
+    def fill_rest(n, carry):
+        pick(step_of(n), range(1, kv_heads))
+        return carry
+
     own_steps = kv_heads * steps
-    lax.fori_loop(0, seq_count - 1, fill, 0)
+    lax.fori_loop(0, seq_count - 1, fill_first, 0)
+    lax.fori_loop(0, 1, fill_rest, 0)
+
+    @pl.when(core == 0)
+    def _():
+        kv_copy(step_of(seq_count - 2), 0).start()
+
+    lax.fori_loop(1, seq_count - 1, fill_rest, 0)
 
     @pl.when(core == 0)
     def _():
@@ -364,12 +392,19 @@
 
     far_kext()
 
+    def wait_blocks(h, first, end, sem):
+        part = pl.ds(first - 1, end - first)
+        pltpu.make_async_remote_copy(
+            src_ref=stage.at[part, h],
+            dst_ref=land.at[part, h],
+            send_sem=kv_ssem,
+            recv_sem=kv_rsem.at[sem],
+            device_id=other("seq", own, seq_count),
+            device_id_type=MESH,
+        ).wait_recv()
+
     def wait_head(h):
-        def arrive(d, carry):
-            kv_copy(d, h).wait_recv()
-            return carry
-
-        lax.fori_loop(1, seq_count, arrive, 0)
+        wait_blocks(h, 1, seq_count, h)
 
     def one_head(h, carry):
         wait_head(h)
@@ -380,7 +415,6 @@
 
         return lax.fori_loop(0, steps, one_row, carry)
 
-    last = kv_heads - 1
     before_last = max(last - 1, 0)
     lax.fori_loop(0, before_last, one_head, 0)
     for h in range(before_last, last):
@@ -391,8 +425,23 @@
     def _():
         pl.semaphore_signal(turn_sem, inc=1, device_id={"dp": core + 1}, device_id_type=MESH)
 
-    wait_head(last)
     loads[5].wait()
+
+    early = last * width
+    if early:
+        for o in range(others):
+            target = lax.rem(head + o + 1, head_count)
+            for at in range(0, cols, piece):
+                start = pl.multiple_of(target * cols + at, piece)
+                first_share[o, :, at : at + piece] = jnp.dot(
+                    attn[0:BLOCK, :early],
+                    w_ref[:early, pl.ds(start, piece)],
+                    preferred_element_type=jnp.float32,
+                )
+
+    wait_blocks(last, 1, middle, last)
+    attend(last, [0], far_slots[: middle - 1], False)
+    wait_blocks(last, middle, seq_count, kv_heads)
 
     def project(i, target, at, size, put):
         rows = attn[pl.ds(pl.multiple_of(i * BLOCK, BLOCK), BLOCK), :]
@@ -403,8 +452,8 @@
         return pltpu.make_async_remote_copy(
             src_ref=ysend.at[o, i, p],
             dst_ref=yrecv.at[o, i, p],
-            send_sem=y_ssem.at[o, i, p],
-            recv_sem=y_rsem.at[o, i, p],
+            send_sem=y_ssem,
+            recv_sem=y_rsem.at[o, jnp.where(i < blocks - 1, i, blocks - 1 + p)],
             device_id={"head": lax.rem(head + o + 1, head_count)},
             device_id_type=MESH,
         )
@@ -423,7 +472,20 @@
                     at = (p - group[0]) * piece
                     ysend[o, i, p] = x[:, at : at + piece].astype(jnp.bfloat16)
 
-            project(i, target, group[0] * piece, len(group) * piece, put)
+            if isinstance(i, int) and early:
+                at = group[0] * piece
+                size_here = len(group) * piece
+                start = pl.multiple_of(target * cols + at, size_here)
+                put(
+                    first_share[o, :, at : at + size_here]
+                    + jnp.dot(
+                        attn[0:BLOCK, early:],
+                        w_ref[early:, pl.ds(start, size_here)],
+                        preferred_element_type=jnp.float32,
+                    )
+                )
+            else:
+                project(i, target, group[0] * piece, len(group) * piece, put)
             if n > 0:
                 for p in groups[n - 1][1]:
                     y_copy(groups[n - 1][0], i, p).start()
@@ -449,7 +511,7 @@
         share(i, 2)
         return carry
 
-    attend(last, [0])
+    attend(last, [0], far_slots[middle - 1 :])
     first_rest = share(0, 1)
     rest = (others - 1, range((pieces - 1) // 2 * 2, pieces))
     lax.fori_loop(1, blocks, tail_row, 0)
@@ -460,7 +522,7 @@
         rows = pl.ds(pl.multiple_of(i * BLOCK, BLOCK), BLOCK)
 
         def put(x):
-            kept[rows, pl.ds(at, tile)] = x
+            kept[rows, pl.ds(at, tile)] = x.astype(jnp.bfloat16)
 
         project(i, head, at, tile, put)
 
@@ -472,28 +534,52 @@
 
     lax.fori_loop(0, blocks * own_tiles, own_share, 0)
 
-    for d in range(1, seq_count):
-        note_copy(d).wait_send()
-
-    def sent(n, carry):
-        kv_copy(n // kv_heads + 1, lax.rem(n, kv_heads)).wait_send()
+    def all_sent(src, dst, sem, unused, axis, at, count):
+        pltpu.make_async_remote_copy(
+            src_ref=src,
+            dst_ref=dst,
+            send_sem=sem,
+            recv_sem=unused,
+            device_id=other(axis, at, count),
+            device_id_type=MESH,
+        ).wait_send()
+
+    all_sent(note_out, note_in, note_ssem, note_rsem.at[0], "seq", own, seq_count)
+    all_sent(stage, land, kv_ssem, kv_rsem.at[0], "seq", own, seq_count)
+
+    def out_copy(rows, part):
+        return pltpu.make_async_copy(kept.at[rows, part], out_hbm.at[rows, part], out_sem)
+
+    def add(rows, i, p):
+        part = slice(p * piece, (p + 1) * piece)
+        total = kept[rows, part].astype(jnp.float32)
+        for o in range(others):
+            total = total + yrecv[o, i, p].astype(jnp.float32)
+        kept[rows, part] = total.astype(jnp.bfloat16)
+        out_copy(rows, pl.ds(p * piece, piece)).start()
+
+    def finish(i, carry):
+        for o in range(others):
+            pltpu.make_async_remote_copy(
+                src_ref=ysend.at[o, i],
+                dst_ref=yrecv.at[o, i],
+                send_sem=y_ssem,
+                recv_sem=y_rsem.at[o, i],
+                device_id=other("head", head, head_count),
+                device_id_type=MESH,
+            ).wait_recv()
+        for p in range(pieces):
+            add(pl.ds(pl.multiple_of(i * BLOCK, BLOCK), BLOCK), i, p)
         return carry
 
-    lax.fori_loop(0, (seq_count - 1) * kv_heads, sent, 0)
-
-    def finish(i, carry):
-        rows = pl.ds(pl.multiple_of(i * BLOCK, BLOCK), BLOCK)
-        for p in range(pieces):
-            total = kept[rows, p * piece : (p + 1) * piece]
-            for o in range(others):
-                y_copy(o, i, p).wait_recv()
-                total = total + yrecv[o, i, p].astype(jnp.float32)
-            out_ref[rows, p * piece : (p + 1) * piece] = total.astype(jnp.bfloat16)
-            for o in range(others):
-                y_copy(o, i, p).wait_send()
-        return carry
-
-    lax.fori_loop(0, blocks, finish, 0)
+    lax.fori_loop(0, blocks - 1, finish, 0)
+    for p in range(pieces):
+        for o in range(others):
+            y_copy(o, blocks - 1, p).wait_recv()
+        add(pl.ds((blocks - 1) * BLOCK, BLOCK), blocks - 1, p)
+
+    all_sent(ysend, yrecv, y_ssem, y_rsem.at[0, 0], "head", head, head_count)
+    pltpu.make_async_copy(kept, out_hbm, out_sem).wait()
 
 
 def per_device(queries, keys, values, doc_ids, block_lists, w_out):
@@ -521,7 +607,7 @@
             hbm,
         ]
         * 6,
-        out_specs=pl.BlockSpec(memory_space=pltpu.VMEM),
+        out_specs=hbm,
         scratch_shapes=[
             pltpu.SMEM(block_lists.shape, i32),
             pltpu.VMEM((blocks, BLOCK), i32),
@@ -529,7 +615,7 @@
             pltpu.VMEM((tokens, kv_width), bf16),
             pltpu.VMEM((tokens, kv_width), bf16),
             pltpu.VMEM(w_out.shape, bf16),
-            pltpu.VMEM((note_rows, LANES), i32),
+            pltpu.VMEM((far, note_rows, LANES), i32),
             pltpu.VMEM((far, note_rows, LANES), i32),
             pltpu.VMEM((far, kv_heads, 2 * BLOCK, HEAD_SIZE), bf16),
             pltpu.VMEM((far, kv_heads, 2 * BLOCK, HEAD_SIZE), bf16),
@@ -540,16 +626,18 @@
             pltpu.VMEM((tokens, depth), bf16),
             pltpu.VMEM((others, blocks, pieces, BLOCK, cols // pieces), bf16),
             pltpu.VMEM((others, blocks, pieces, BLOCK, cols // pieces), bf16),
-            pltpu.VMEM((tokens, cols), f32),
+            pltpu.VMEM((tokens, cols), bf16),
             pltpu.VMEM((kv_heads * blocks, 2, half, 2 * LANES), f32),
             pltpu.VMEM((kv_heads * blocks, 2, half, LANES), f32),
+            pltpu.VMEM((others, BLOCK, cols), f32),
             pltpu.SemaphoreType.DMA((6,)),
+            pltpu.SemaphoreType.DMA,
             pltpu.SemaphoreType.DMA((far,)),
-            pltpu.SemaphoreType.DMA((far,)),
-            pltpu.SemaphoreType.DMA((far, kv_heads)),
-            pltpu.SemaphoreType.DMA((far, kv_heads)),
-            pltpu.SemaphoreType.DMA((others, blocks, pieces)),
-            pltpu.SemaphoreType.DMA((others, blocks, pieces)),
+            pltpu.SemaphoreType.DMA,
+            pltpu.SemaphoreType.DMA((kv_heads + 1,)),
+            pltpu.SemaphoreType.DMA,
+            pltpu.SemaphoreType.DMA((others, blocks - 1 + pieces)),
+            pltpu.SemaphoreType.DMA,
             pltpu.SemaphoreType.REGULAR,
         ],
         compiler_params=pltpu.CompilerParams(

time: 84.5 us -> 83.5 us (0.988)
  Pallas kernels: 83 us -> 82 us
    pallas_call x1, Pallas kernels: 83 us -> 82 us  [per_device(): pl.pallas_call(functools.partial(kernel, seq_count, head_count, dp_count)...]
where the time goes in v3:
time: 83.5 us; the launch traced here: 83.3 us
  Pallas kernels  82 us (98%)
  local copies, waits for them, and re-layouts  1.32 us (2%)
    pallas_call x1, Pallas kernels, per_device(): pl.pallas_call(functools.partial(kernel, seq_count, head_count, dp_count)...  82 us

profile of v3, /device:TPU:1, one launch (start us, length us, event | category | flops | bytes accessed | tf_op | source)
XLA Modules:
  0.0 83.3 jit_solution(2838879884176824342)
XLA Ops:
  0.0 82.0 %shard_map.64 = bf16[512,2048]{1,0:T(8,128)(2,1)S(1)} custom-call(s32[4,16]{1,0:T(4,128)} %lists_hbm.1, s32[4,128]{1,0:T(4,128)} %bitcast.1, bf16[512,2048]{1,0:T(8,128)(2,1)} %q_hbm.1, bf16[512,512]{1,0:T(8,128)(2,1)} %k_hbm.1, bf16[512,512]{1,0:T(8,128)(2,1)} %v_hbm.1, bf16[2048,4096]{1,0:T(8,128)(2,1)} %w_hbm.1), custom_call_target="tpu_custom_call" | custom-call | tf_op jit(solution)/shard_map/pallas_call | solution.py:603
  82.0 1.3 %copy.8 = bf16[512,2048]{1,0:T(8,128)(2,1)} copy(bf16[512,2048]{1,0:T(8,128)(2,1)S(1)} %shard_map.64) | data formatting | bytes 4194304

commit v4 on v3

--- a/solution.py
+++ b/solution.py
@@ -185,7 +185,8 @@
     def send_heads(first):
         def send_head(h, carry):
             def send(n, inner):
-                kv_copy(n + 1, h).start()
+                d = jnp.where(core == 0, n + 1, step_of(seq_count - 2 - n))
+                kv_copy(d, h).start()
                 return inner
 
             return lax.fori_loop(0, seq_count - 1, send, carry)
@@ -547,16 +548,19 @@
     all_sent(note_out, note_in, note_ssem, note_rsem.at[0], "seq", own, seq_count)
     all_sent(stage, land, kv_ssem, kv_rsem.at[0], "seq", own, seq_count)
 
-    def out_copy(rows, part):
+    def block_rows(i):
+        return pl.ds(pl.multiple_of(i * BLOCK, BLOCK), BLOCK)
+
+    def out_copy(i, part):
+        rows = block_rows(i)
         return pltpu.make_async_copy(kept.at[rows, part], out_hbm.at[rows, part], out_sem)
 
-    def add(rows, i, p):
-        part = slice(p * piece, (p + 1) * piece)
+    def add(i, p):
+        rows, part = block_rows(i), slice(p * piece, (p + 1) * piece)
         total = kept[rows, part].astype(jnp.float32)
         for o in range(others):
             total = total + yrecv[o, i, p].astype(jnp.float32)
         kept[rows, part] = total.astype(jnp.bfloat16)
-        out_copy(rows, pl.ds(p * piece, piece)).start()
 
     def finish(i, carry):
         for o in range(others):
@@ -569,16 +573,27 @@
                 device_id_type=MESH,
             ).wait_recv()
         for p in range(pieces):
-            add(pl.ds(pl.multiple_of(i * BLOCK, BLOCK), BLOCK), i, p)
+            add(i, p)
+
+        @pl.when(i > 0)
+        def _():
+            out_copy(i - 1, pl.ds(0, cols)).start()
+
         return carry
 
-    lax.fori_loop(0, blocks - 1, finish, 0)
+    end = blocks - 1
+    lax.fori_loop(0, end, finish, 0)
     for p in range(pieces):
         for o in range(others):
-            y_copy(o, blocks - 1, p).wait_recv()
-        add(pl.ds((blocks - 1) * BLOCK, BLOCK), blocks - 1, p)
+            y_copy(o, end, p).wait_recv()
+        add(end, p)
+        if p > 0:
+            out_copy(end, pl.ds((p - 1) * piece, piece)).start()
+        elif end > 0:
+            out_copy(end - 1, pl.ds(0, cols)).start()
 
     all_sent(ysend, yrecv, y_ssem, y_rsem.at[0, 0], "head", head, head_count)
+    out_copy(end, pl.ds((pieces - 1) * piece, piece)).start()
     pltpu.make_async_copy(kept, out_hbm, out_sem).wait()
 
 

time: 83.5 us -> 83.5 us (level)
  no operation moved by 1% of the time
where the time goes in v4:
time: 83.5 us; the launch traced here: 83.3 us
  Pallas kernels  82 us (98%)
  local copies, waits for them, and re-layouts  1.32 us (2%)
    pallas_call x1, Pallas kernels, per_device(): pl.pallas_call(functools.partial(kernel, seq_count, head_count, dp_count)...  82 us

profile of v4, /device:TPU:1, one launch (start us, length us, event | category | flops | bytes accessed | tf_op | source)
XLA Modules:
  0.0 83.3 jit_solution(11130089805516005113)
XLA Ops:
  0.0 82.0 %shard_map.64 = bf16[512,2048]{1,0:T(8,128)(2,1)S(1)} custom-call(s32[4,16]{1,0:T(4,128)} %lists_hbm.1, s32[4,128]{1,0:T(4,128)} %bitcast.1, bf16[512,2048]{1,0:T(8,128)(2,1)} %q_hbm.1, bf16[512,512]{1,0:T(8,128)(2,1)} %k_hbm.1, bf16[512,512]{1,0:T(8,128)(2,1)} %v_hbm.1, bf16[2048,4096]{1,0:T(8,128)(2,1)} %w_hbm.1), custom_call_target="tpu_custom_call" | custom-call | tf_op jit(solution)/shard_map/pallas_call | solution.py:618
  82.0 1.3 %copy.8 = bf16[512,2048]{1,0:T(8,128)(2,1)} copy(bf16[512,2048]{1,0:T(8,128)(2,1)S(1)} %shard_map.64) | data formatting | bytes 4194304
